TPU v7x, 128 devices: a whole 4x4x4 slice. The times are simulated.
128 devices in a mesh: dp: 1, sp: 128 (over z, y, x, core).
Axes of the slice: x: 4, y: 4, z: 4, core: 2. Of those that a mesh axis runs over, the one named last changes fastest.
Arguments:
- z_points: bfloat16 [262144, 384], P(('dp', 'sp'))
- x_points: bfloat16 [16384, 384], P(('dp', 'sp'))
- rhs_vals: bfloat16 [16384, 64], P(('dp', 'sp'))
- block_mask: int32 [128, 128], P(('dp', 'sp'))
- length_scale: float32 [1], replicated
- out_scale: float32 [1], replicated
Outputs:
- output: float32 [262144, 64], P(('dp', 'sp'))
All inputs are finite; a program needn't handle non-finite values.
Results may differ from a plain program's by a relative error of at most 0.001.
Values are sent between devices in bfloat16 or wider.
A program may use at most 1 GiB of HBM per device.

v0:
```python
import jax
import jax.numpy as jnp
from jax import lax
from jax.sharding import PartitionSpec as P


def block_product(z_rows, z_norm, x_rows, v_rows, ell_sq, scale_val):
    x_norm = jnp.einsum("nd,nd->n", x_rows, x_rows, preferred_element_type=jnp.float32)
    gram_blk = jnp.einsum("md,nd->mn", z_rows, x_rows, preferred_element_type=jnp.float32)
    sq_dist = jnp.maximum(z_norm[:, None] + x_norm[None, :] - 2.0 * gram_blk, 0.0)
    kern_blk = (scale_val * jnp.exp(-sq_dist / (2.0 * ell_sq))).astype(jnp.bfloat16)
    return jnp.dot(kern_blk, v_rows, preferred_element_type=jnp.float32)


def solution(mesh):
    group_size = mesh.shape["sp"]
    shift_pairs = [(dev_idx, (dev_idx + 1) % group_size) for dev_idx in range(group_size)]
    row_spec = P(("dp", "sp"), None)

    def local_fn(z_rows, x_rows, v_rows, mask_row, length_scale, out_scale):
        my_index = lax.axis_index("sp")
        ell_sq = length_scale[0] * length_scale[0]
        scale_val = out_scale[0]
        weights = mask_row[0].astype(jnp.float32)
        z_norm = jnp.einsum("md,md->m", z_rows, z_rows, preferred_element_type=jnp.float32)
        first_y = block_product(z_rows, z_norm, x_rows, v_rows, ell_sq, scale_val) * weights[my_index]

        def shift_step(step_idx, loop_state):
            x_cur, v_cur, y_acc = loop_state
            x_cur = lax.ppermute(x_cur, "sp", shift_pairs)
            v_cur = lax.ppermute(v_cur, "sp", shift_pairs)
            src_block = (my_index - step_idx) % group_size
            part_y = block_product(z_rows, z_norm, x_cur, v_cur, ell_sq, scale_val)
            return (x_cur, v_cur, y_acc + part_y * weights[src_block])

        final_state = lax.fori_loop(1, group_size, shift_step, (x_rows, v_rows, first_y))
        return final_state[2]

    return jax.shard_map(local_fn, mesh=mesh, in_specs=(row_spec, row_spec, row_spec, row_spec, P(None), P(None)), out_specs=row_spec, check_vma=False)
```

profile of v0, /device:TPU:1, one launch (start us, length us, event | category | flops | bytes accessed | tf_op | source)
XLA Modules:
  0.0 1533.7 jit_solution(1649271883879076984)
XLA Ops:
  7.8 1525.1 %while.19 = (s32[]{:T(128)}, bf16[128,384]{1,0:T(8,128)(2,1)S(1)}, bf16[128,64]{0,1:T(8,128)(2,1)S(1)}, f32[2048,64]{0,1:T(8,128)S(1)}, f32[]{:T(128)}, /*index=...) while((s32[]{:T(128)}, bf16[128,384]{1,0:T(8,128)(2,1)S(1)}, ...), condition=%wide.region_1.2_spmd, body=%wide.region_0.1_spmd.sunk | while | flops 237387664 | bytes 3532168 | solution.py:36
  26.3 8.9 collective-permute-done.1
  38.4 8.9 collective-permute-done.1
  50.4 8.9 collective-permute-done.1
  62.5 8.9 collective-permute-done.1
  74.6 8.9 collective-permute-done.1
  86.6 8.9 collective-permute-done.1
  98.7 8.9 collective-permute-done.1
  110.7 8.9 collective-permute-done.1
  122.8 8.9 collective-permute-done.1
  134.9 8.9 collective-permute-done.1
  146.9 8.9 collective-permute-done.1
  159.0 8.9 collective-permute-done.1
  171.0 8.9 collective-permute-done.1
  183.1 8.9 collective-permute-done.1
  195.2 8.9 collective-permute-done.1
  219.3 8.9 collective-permute-done.1
  231.3 8.9 collective-permute-done.1
  243.4 8.9 collective-permute-done.1
  255.4 8.9 collective-permute-done.1
  267.5 8.9 collective-permute-done.1
  279.6 8.9 collective-permute-done.1
  291.6 8.9 collective-permute-done.1
  303.7 8.9 collective-permute-done.1
  315.7 8.9 collective-permute-done.1
  327.8 8.9 collective-permute-done.1
  339.9 8.9 collective-permute-done.1
  351.9 8.9 collective-permute-done.1
  364.0 8.9 collective-permute-done.1
  376.0 8.9 collective-permute-done.1
  388.1 8.9 collective-permute-done.1
  400.2 8.9 collective-permute-done.1
  412.2 8.9 collective-permute-done.1
  424.3 8.9 collective-permute-done.1
  448.4 8.9 collective-permute-done.1
  460.4 8.9 collective-permute-done.1
  472.5 8.9 collective-permute-done.1
  484.6 8.9 collective-permute-done.1
  496.6 8.9 collective-permute-done.1
  508.7 8.9 collective-permute-done.1
  520.7 8.9 collective-permute-done.1
  532.8 8.9 collective-permute-done.1
  544.9 8.9 collective-permute-done.1
  556.9 8.9 collective-permute-done.1
  569.0 8.9 collective-permute-done.1
  581.0 8.9 collective-permute-done.1
  593.1 8.9 collective-permute-done.1
  605.2 8.9 collective-permute-done.1
  (1107 shorter events, 1104.6 us)
Async XLA Ops:
  25.5 9.7 collective-permute-start
  37.6 9.7 collective-permute-start
  49.6 9.7 collective-permute-start
  61.7 9.7 collective-permute-start
  73.8 9.7 collective-permute-start
  85.8 9.7 collective-permute-start
  97.9 9.7 collective-permute-start
  109.9 9.7 collective-permute-start
  122.0 9.7 collective-permute-start
  134.1 9.7 collective-permute-start
  146.1 9.7 collective-permute-start
  158.2 9.7 collective-permute-start
  170.2 9.7 collective-permute-start
  182.3 9.7 collective-permute-start
  194.3 9.7 collective-permute-start
  206.4 9.7 collective-permute-start
  218.5 9.7 collective-permute-start
  230.5 9.7 collective-permute-start
  242.6 9.7 collective-permute-start
  254.6 9.7 collective-permute-start
  266.7 9.7 collective-permute-start
  278.8 9.7 collective-permute-start
  290.8 9.7 collective-permute-start
  302.9 9.7 collective-permute-start
  314.9 9.7 collective-permute-start
  327.0 9.7 collective-permute-start
  339.1 9.7 collective-permute-start
  351.1 9.7 collective-permute-start
  363.2 9.7 collective-permute-start
  375.2 9.7 collective-permute-start
  387.3 9.7 collective-permute-start
  399.4 9.7 collective-permute-start
  411.4 9.7 collective-permute-start
  423.5 9.7 collective-permute-start
  435.5 9.7 collective-permute-start
  447.6 9.7 collective-permute-start
  459.6 9.7 collective-permute-start
  471.7 9.7 collective-permute-start
  483.8 9.7 collective-permute-start
  495.8 9.7 collective-permute-start
  507.9 9.7 collective-permute-start
  519.9 9.7 collective-permute-start
  532.0 9.7 collective-permute-start
  544.1 9.7 collective-permute-start
  556.1 9.7 collective-permute-start
  568.2 9.7 collective-permute-start
  580.2 9.7 collective-permute-start
  592.3 9.7 collective-permute-start
  (208 other events, 1980.4 us)
where the time goes:
time: 1540 us; the launch traced here: 1530 us
  waiting for transfers between devices  1120 us (73%)
  matrix products  279 us (18%)
  local copies, waits for them, and re-layouts  83.3 us (5%)
  starting transfers between devices  24 us (2%)
  other arithmetic  15.9 us (1%)
    ppermute x127, waiting for transfers between devices, shift_step(): v_cur = lax.ppermute(v_cur, 'sp', shift_pairs)  1120 us
    dot_general x128, matrix products, block_product(): return jnp.dot(kern_blk, v_rows, preferred_element_type=jnp.float32)  279 us
    dynamic_slice x127, local copies, waits for them, and re-layouts, shift_step(): return (x_cur, v_cur, y_acc + part_y * weights[src_block])  77.9 us
  transfers between devices with their start and end apart: 254, of which 127 were waited for; matrix products, arithmetic and copies ran while one was open for 5% of the time, Pallas kernels for 0%

commit v1 on v0

v1 whole, which is shorter than its diff:
```python
import functools

import jax
import jax.numpy as jnp
from jax import lax
from jax.experimental import pallas as pl
from jax.experimental.pallas import tpu as pltpu
from jax.sharding import PartitionSpec as P

MESH = pl.DeviceIdType.MESH
F32 = jnp.float32
BF16 = jnp.bfloat16
LOG2E = 1.4426950408889634
ROWS = 128
PIECES = ((0, 48), (48, 48), (96, 32))
GROUP = 4
TILES = 4
EARLY = 2


def item_order(ring):
    hops = [(i, j, k) for i in range(ring) for j in range(ring) for k in range(ring)]
    return sorted(hops, key=lambda h: (sum(h), h[2], h[1], h[0]))


def split3(val):
    hi = val.astype(BF16).astype(F32)
    rest = val - hi
    mid = rest.astype(BF16).astype(F32)
    return hi, mid, (rest - mid).astype(BF16).astype(F32)


def kernel(ring, x_hbm, z_hbm, w_ref, ell_ref, scale_ref, y_ref,
           xb, zv, zt, aug, vt, ks, wsm, in_sem, recv_sem, pair_sem, send_sem):
    order = item_order(ring)
    slot_of = {h: n for n, h in enumerate(order)}
    n_items = len(order)
    n_groups = n_items // GROUP
    half = GROUP * ROWS
    tile = zv.shape[0] // TILES

    me = lax.axis_index("sp")
    core = me % 2
    pos = [(me // 2) % ring, (me // (2 * ring)) % ring, me // (2 * ring * ring)]
    step = 1 - 2 * core
    shifted = [[(p + (ring - h) * step + ring * ring) % ring for h in range(ring)] for p in pos]

    def device(x, y, z, c):
        return ((z * ring + y) * ring + x) * 2 + c

    downstream, upstream = [], []
    for axis in range(3):
        for lst, hop in ((downstream, ring - 1), (upstream, 1)):
            at = [shifted[a][hop] if a == axis else pos[a] for a in range(3)]
            lst.append(device(*at, core))
    partner = me + step

    own_in = pltpu.make_async_copy(x_hbm, xb.at[0], in_sem.at[0])
    z_in = pltpu.make_async_copy(z_hbm, zv, in_sem.at[1])
    own_in.start()
    z_in.start()
    barrier = pltpu.get_barrier_semaphore()
    for other in (*downstream, *upstream, partner):
        pl.semaphore_signal(barrier, inc=1, device_id={"sp": other}, device_id_type=MESH)
    pl.semaphore_wait(barrier, 7)
    own_in.wait()

    def slot_index(n):
        return (n // GROUP) * 2 * GROUP + n % GROUP

    sent = [0] * n_groups

    def forward(n):
        i, j, k = order[n]
        src = slot_index(n)
        for leg in range(3):
            if leg == 0:
                child = (i + 1, j, k) if j == 0 and k == 0 else None
            elif leg == 1:
                child = (i, j + 1, k) if k == 0 else None
            else:
                child = (i, j, k + 1)
            if child is None or child not in slot_of:
                continue
            m = slot_of[child]
            for colour, (lo, cnt) in enumerate(PIECES):
                pltpu.make_async_remote_copy(
                    src_ref=xb.at[src, pl.ds(lo, cnt)],
                    dst_ref=xb.at[slot_index(m), pl.ds(lo, cnt)],
                    send_sem=send_sem.at[n // GROUP],
                    recv_sem=recv_sem.at[m],
                    device_id={"sp": downstream[(colour + leg) % 3]},
                    device_id_type=MESH,
                ).start()
            sent[n // GROUP] += 1

    def arrive(n):
        dst = xb.at[slot_index(n)]
        pltpu.make_async_copy(dst, dst, recv_sem.at[n]).wait()

    def to_partner(q):
        pltpu.make_async_remote_copy(
            src_ref=xb.at[pl.ds(2 * GROUP * q, GROUP)],
            dst_ref=xb.at[pl.ds(2 * GROUP * (q + 1) + GROUP, GROUP)],
            send_sem=send_sem.at[q],
            recv_sem=pair_sem.at[q],
            device_id={"sp": partner},
            device_id_type=MESH,
        ).start()
        sent[q] += GROUP

    def from_partner(q):
        dst = xb.at[pl.ds(2 * GROUP * (q + 1) + GROUP, GROUP)]
        pltpu.make_async_copy(dst, dst, pair_sem.at[q]).wait()

    def mask_words(n, theirs):
        slot = slot_index(n) + (3 * GROUP if theirs else 0)
        for colour in range(3):
            at = [None] * 3
            for leg in range(3):
                axis = (colour + leg) % 3
                hop = order[n][leg]
                at[axis] = shifted[axis][(ring - hop) % ring if theirs else hop]
            wsm[slot * 3 + colour] = w_ref[0, device(*at, 1 - core if theirs else core)]

    lane = lax.broadcasted_iota(jnp.int32, (1, 128), 1)
    lane_full = lax.broadcasted_iota(jnp.int32, (ROWS, 128), 1)

    def prepare(slot, buf, place):
        x = xb[slot, :, 0:384].astype(F32)
        sq = x * x
        nx = jnp.sum(sq[:, 0:128] + sq[:, 128:256] + sq[:, 256:384], axis=1, keepdims=True)
        hi, mid, low = split3(-0.5 * nx)
        cols = jnp.where(lane_full < 3, 1.0, 0.0)
        cols = jnp.where(lane_full == 3, hi, cols)
        cols = jnp.where(lane_full == 4, mid, cols)
        cols = jnp.where(lane_full == 5, low, cols)
        base = pl.multiple_of(place * ROWS, ROWS)
        aug[buf, pl.ds(base, ROWS), :] = cols.astype(BF16)
        w = jnp.where(lane < 48, wsm[slot * 3], jnp.where(lane < 96, wsm[slot * 3 + 1], wsm[slot * 3 + 2]))
        v_t = xb[slot, :, 384:512].T[0:64, :]
        vt[buf, :, pl.ds(base, ROWS)] = (v_t.astype(F32) * w.astype(F32)).astype(BF16)

    forward(0)
    for n in range(GROUP):
        mask_words(n, False)

    vt[...] = jnp.zeros_like(vt)
    ks[...] = jnp.zeros_like(ks)
    y_ref[...] = jnp.zeros_like(y_ref)
    z_in.wait()
    row = lax.broadcasted_iota(jnp.int32, (128, tile), 0)

    def prepare_targets(r, carry):
        base = pl.multiple_of(r * tile, tile)
        zr = zv[pl.ds(base, tile), :].T
        zt[0:384, pl.ds(base, tile)] = zr
        zf = zr.astype(F32)
        hi, mid, low = split3(-0.5 * jnp.sum(zf * zf, axis=0, keepdims=True))
        rows = jnp.where(row == 0, hi, jnp.where(row == 1, mid, jnp.where(row == 2, low, 0.0)))
        rows = jnp.where((row >= 3) & (row < 6), 1.0, rows)
        zt[384:512, pl.ds(base, tile)] = rows.astype(BF16)
        return carry

    lax.fori_loop(0, TILES, prepare_targets, 0)
    ell = jnp.full((1, tile), ell_ref[0], F32)
    rate = LOG2E / (ell * ell)
    scale = scale_ref[0]

    prepare(0, 0, 0)
    for n in range(1, GROUP):
        arrive(n)
        forward(n)
    to_partner(0)
    for n in range(1, GROUP):
        prepare(slot_index(n), 0, n)

    def product(buf, prev, at):
        base = pl.multiple_of(at * tile, tile)
        y_ref[:, pl.ds(base, tile)] += jnp.dot(vt[buf], ks[prev], preferred_element_type=F32)

    def run_chunk(g, prep):
        first = 2 * GROUP * g + (GROUP if g == n_groups else 0)
        count = GROUP if g in (0, n_groups) else 2 * GROUP
        rows = count * ROWS

        def body(r, carry):
            now = r % 2
            src = xb[pl.ds(first, count)].reshape(rows, 512)[:, 0:384]
            lhs = jnp.concatenate([src, aug[g % 3, 0:rows, :]], axis=1)
            base = pl.multiple_of(r * tile, tile)
            neg = jnp.dot(lhs, zt[:, pl.ds(base, tile)], preferred_element_type=F32)
            val = jnp.exp2(jnp.minimum(neg * rate, 0.0)) * scale
            ks[now, 0:rows, :] = val.astype(BF16)
            buf = jnp.where(r == 0, (g + 2) % 3, g % 3)
            product(buf, 1 - now, (r + TILES - 1) % TILES)
            if prep:
                prepare_next(g + 1, r)
            return carry

        lax.fori_loop(0, TILES, body, 0)

    def prepare_next(n, r):
        if n < n_groups:
            prepare(2 * GROUP * n + r, n % 3, r)
        if n >= 1:
            prepare(2 * GROUP * n + GROUP + r, n % 3, r + (0 if n == n_groups else GROUP))

    def communicate(n):
        if n < n_groups:
            for m in range(GROUP * n, GROUP * (n + 1)):
                mask_words(m, False)
                arrive(m)
                forward(m)
            to_partner(n)
        for m in range(GROUP * (n - 1), GROUP * n):
            mask_words(m, True)
        from_partner(n - 1)
        if n == n_groups:
            vt[n % 3, :, half:] = jnp.zeros((64, half), BF16)

    for g in range(n_groups + 1):
        if g == n_groups:
            run_chunk(g, False)
        elif g < EARLY:
            run_chunk(g, False)
            communicate(g + 1)

            def prep_body(r, carry, n=g + 1):
                prepare_next(n, r)
                return carry

            lax.fori_loop(0, GROUP, prep_body, 0)
        else:
            communicate(g + 1)
            run_chunk(g, True)
    product(n_groups % 3, (TILES - 1) % 2, TILES - 1)
    for q in range(n_groups):
        done = xb.at[pl.ds(0, sent[q])]
        pltpu.make_async_copy(done, done, send_sem.at[q]).wait()


def solution(mesh):
    devices = mesh.shape["sp"]
    ring = round((devices // 2) ** (1 / 3))
    n_items = ring**3
    n_groups = n_items // GROUP
    row_spec = P(("dp", "sp"), None)

    def local_fn(z_rows, x_rows, v_rows, mask_row, length_scale, out_scale):
        targets = z_rows.shape[0]
        tile = targets // TILES
        pad = jnp.zeros((ROWS, 128 - v_rows.shape[1]), BF16)
        packed = jnp.concatenate([x_rows, v_rows, pad], axis=1)
        y_t = pl.pallas_call(
            functools.partial(kernel, ring),
            out_shape=jax.ShapeDtypeStruct((64, targets), F32),
            in_specs=[
                pl.BlockSpec(memory_space=pl.ANY),
                pl.BlockSpec(memory_space=pl.ANY),
                pl.BlockSpec(memory_space=pltpu.SMEM),
                pl.BlockSpec(memory_space=pltpu.SMEM),
                pl.BlockSpec(memory_space=pltpu.SMEM),
            ],
            out_specs=pl.BlockSpec(memory_space=pltpu.VMEM),
            scratch_shapes=[
                pltpu.VMEM((2 * GROUP * (n_groups + 1), ROWS, 512), BF16),
                pltpu.VMEM((targets, 384), BF16),
                pltpu.VMEM((512, targets), BF16),
                pltpu.VMEM((3, 2 * GROUP * ROWS, 128), BF16),
                pltpu.VMEM((3, 64, 2 * GROUP * ROWS), BF16),
                pltpu.VMEM((2, 2 * GROUP * ROWS, tile), BF16),
                pltpu.SMEM((2 * GROUP * (n_groups + 1) * 3,), jnp.int32),
                pltpu.SemaphoreType.DMA((2,)),
                pltpu.SemaphoreType.DMA((n_items,)),
                pltpu.SemaphoreType.DMA((n_groups,)),
                pltpu.SemaphoreType.DMA((n_groups,)),
            ],
            compiler_params=pltpu.CompilerParams(
                collective_id=0, has_side_effects=True, vmem_limit_bytes=60 * 2**20
            ),
            name="gather_product",
        )(packed, z_rows, mask_row, length_scale, out_scale)
        return y_t.T

    return jax.shard_map(
        local_fn,
        mesh=mesh,
        in_specs=(row_spec, row_spec, row_spec, row_spec, P(None), P(None)),
        out_specs=row_spec,
        check_vma=False,
    )
```

time: 1540 us -> 105 us (0.07)
  waiting for transfers between devices: 1120 us -> 0 us
  matrix products: 279 us -> 0 us
  Pallas kernels: 0 us -> 98.6 us
  local copies, waits for them, and re-layouts: 83.3 us -> 2.78 us
  starting transfers between devices: 24 us -> 0 us
    ppermute x254 -> x0, waiting for transfers between devices: 1120 us -> none  [the longest x127 1120 us: shift_step(): v_cur = lax.ppermute(v_cur, 'sp', shift_pairs)]
    dot_general x128 -> x0, matrix products: 279 us -> none  [block_product(): return jnp.dot(kern_blk, v_rows, preferred_element_type=jnp.float32)]
    pallas_call x0 -> x1, Pallas kernels: none -> 98.6 us  [local_fn(): pl.pallas_call(functools.partial(kernel, ring), out_shape=jax.ShapeDtypeS...]
    dynamic_slice x128 -> x0, local copies, waits for them, and re-layouts: 78.5 us -> none  [the longest x127 77.9 us: shift_step(): return (x_cur, v_cur, y_acc + part_y * weights[src_block])]
    ppermute x254 -> x0, starting transfers between devices: 24 us -> none  [the longest x127 14.5 us: shift_step(): x_cur = lax.ppermute(x_cur, 'sp', shift_pairs)]
  transfers between devices with their start and end apart: 254 -> 0, of which waited for: 127 -> 0; matrix products, arithmetic and copies ran while one was open for 5% -> 0% of each run, Pallas kernels for 0% -> 0%
where the time goes in v1:
time: 105 us; the launch traced here: 104 us
  Pallas kernels  98.6 us (94%)
  local copies, waits for them, and re-layouts  2.78 us (3%)
  other arithmetic  1.58 us (2%)
  between operations  1.32 us (1%)
    pallas_call x1, Pallas kernels, local_fn(): pl.pallas_call(functools.partial(kernel, ring), out_shape=jax.ShapeDtypeS...  98.6 us
    unnamed x2, local copies, waits for them, and re-layouts  2.7 us

profile of v1, /device:TPU:1, one launch (start us, length us, event | category | flops | bytes accessed | tf_op | source)
XLA Modules:
  0.0 104.3 jit_solution(11707764051504346143)
XLA Ops:
  1.3 0.1 pad.2.clone
  1.4 0.8 copy.7
  2.2 1.6 %maximum_maximum_fusion.x_hbm = bf16[128,512]{1,0:T(8,128)(2,1)} fusion(bf16[128,64]{1,0:T(8,128)(2,1)S(1)} %copy.7, bf16[128,384]{1,0:T(8,128)(2,1)} %param.7, bf16[512]{0:T(512)(128)(2,1)S(1)} %pad.2.clone), kind=kLoop, calls=%fused_computation | loop fusion | flops 393216 | bytes 246784 | tf_op jit(solution)/shard_map/concatenate | solution.py:254
  3.8 98.6 %gather_product.1 = f32[64,2048]{1,0:T(8,128)} custom-call(bf16[128,512]{1,0:T(8,128)(2,1)} %maximum_maximum_fusion.x_hbm, bf16[2048,384]{1,0:T(8,128)(2,1)} %z_hbm.1, s32[1,128]{1,0:T(1,128)} %w_ref.1, f32[1]{0:T(128)S(6)} %copy.9.ell_ref, f32[1]{0:T(128)S(6)} %copy.10.scale_ref), custom_call_target="tpu_custom_call" | custom-call | tf_op jit(solution)/shard_map/gather_product/pallas_call | solution.py:255
  102.4 1.9 %copy.11 = f32[2048,64]{0,1:T(8,128)} copy(f32[2048,64]{0,1:T(8,128)} %bitcast.1) | data formatting | bytes 1048576
  (1 shorter events, 0.0 us)

commit v2 on v1

v2 whole, which is shorter than its diff:
```python
import functools

import jax
import jax.numpy as jnp
from jax import lax
from jax.experimental import pallas as pl
from jax.experimental.pallas import tpu as pltpu
from jax.sharding import PartitionSpec as P

MESH = pl.DeviceIdType.MESH
F32 = jnp.float32
BF16 = jnp.bfloat16
LOG2E = 1.4426950408889634
ROWS = 128
PIECES = ((0, 32, 0, 1), (32, 16, 0, -1), (48, 32, 1, 1), (80, 16, 1, -1), (96, 16, 2, 1), (112, 16, 2, -1))
TILES = 4
EARLY = 1


def line_order(ring):
    hops = [(j, k) for j in range(ring) for k in range(ring)]
    return sorted(hops, key=lambda h: (sum(h), h[1], h[0]))


def split3(val):
    hi = val.astype(BF16).astype(F32)
    rest = val - hi
    mid = rest.astype(BF16).astype(F32)
    return hi, mid, (rest - mid).astype(BF16).astype(F32)


def kernel(ring, x_hbm, z_hbm, w_ref, ell_ref, scale_ref, y_ref,
           xb, zv, zt, aug0, aug1, stage, vt, ks0, ks1, wsm, in_sem, recv_sem, pair_sem, send_sem):
    order = line_order(ring)
    slot_of = {h: n for n, h in enumerate(order)}
    n_groups = len(order)
    half = ring * ROWS
    tile = zv.shape[0] // TILES
    aug = (aug0, aug1)
    per_body = ring // (TILES // 2)

    me = lax.axis_index("sp")
    core = me % 2
    pos = [(me // 2) % ring, (me // (2 * ring)) % ring, me // (2 * ring * ring)]
    step = 1 - 2 * core
    shifted = [[(p + (ring - h) * step + ring * ring) % ring for h in range(ring)] for p in pos]

    def device(coords, c):
        x, y, z = coords
        return ((z * ring + y) * ring + x) * 2 + c

    def upstream(axis, sign, hop):
        return shifted[axis][hop if sign > 0 else (ring - hop) % ring]

    def downstream(axis, sign, hop):
        at = list(pos)
        at[axis] = upstream(axis, sign, (ring - hop) % ring)
        return device(at, core)

    partner = me + step

    own_in = pltpu.make_async_copy(x_hbm, xb.at[0], in_sem.at[0])
    z_in = pltpu.make_async_copy(z_hbm, zv, in_sem.at[1])
    own_in.start()
    z_in.start()
    barrier = pltpu.get_barrier_semaphore()
    others = [downstream(axis, 1, hop) for axis in range(3) for hop in range(1, ring)] + [partner]
    for other in others:
        pl.semaphore_signal(barrier, inc=1, device_id={"sp": other}, device_id_type=MESH)
    pl.semaphore_wait(barrier, len(others))
    own_in.wait()

    sent = [0] * n_groups

    def send(src, dst, axis, sign, hop, q, m):
        pltpu.make_async_remote_copy(
            src_ref=src,
            dst_ref=dst,
            send_sem=send_sem.at[q],
            recv_sem=recv_sem.at[m],
            device_id={"sp": downstream(axis, sign, hop)},
            device_id_type=MESH,
        ).start()

    def send_own():
        for hop in sorted(range(1, ring), key=lambda h: min(h, ring - h)):
            for lo, cnt, rot, sign in PIECES:
                rows = pl.ds(lo, cnt)
                send(xb.at[0, rows], xb.at[hop, rows], rot, sign, hop, 0, 0)
            sent[0] += 1

    def forward(q):
        j, k = order[q]
        for leg, child in ((1, (j + 1, k) if k == 0 else None), (2, (j, k + 1))):
            if child not in slot_of:
                continue
            m = slot_of[child]
            for lo, cnt, rot, sign in PIECES:
                rows = pl.ds(lo, cnt)
                send(
                    xb.at[pl.ds(2 * ring * q, ring), rows],
                    xb.at[pl.ds(2 * ring * m, ring), rows],
                    (rot + leg) % 3, sign, 1, q, m,
                )
            sent[q] += ring

    def arrive(q):
        dst = xb.at[pl.ds(1, ring - 1)] if q == 0 else xb.at[pl.ds(2 * ring * q, ring)]
        pltpu.make_async_copy(dst, dst, recv_sem.at[q]).wait()

    def to_partner(q):
        pltpu.make_async_remote_copy(
            src_ref=xb.at[pl.ds(2 * ring * q, ring)],
            dst_ref=xb.at[pl.ds(2 * ring * (q + 1) + ring, ring)],
            send_sem=send_sem.at[q],
            recv_sem=pair_sem.at[q],
            device_id={"sp": partner},
            device_id_type=MESH,
        ).start()
        sent[q] += ring

    def from_partner(q):
        dst = xb.at[pl.ds(2 * ring * (q + 1) + ring, ring)]
        pltpu.make_async_copy(dst, dst, pair_sem.at[q]).wait()

    def mask_words(q, theirs):
        for i in range(ring):
            slot = (2 * ring * (q + 1) + ring if theirs else 2 * ring * q) + i
            for p, (_, _, rot, sign) in enumerate(PIECES):
                at = [None] * 3
                for leg, hop in enumerate((i, *order[q])):
                    axis = (rot + leg) % 3
                    at[axis] = upstream(axis, -sign if theirs else sign, hop)
                wsm[slot * 6 + p] = w_ref[0, device(at, 1 - core if theirs else core)]

    lane = lax.broadcasted_iota(jnp.int32, (1, 128), 1)
    lane_full = lax.broadcasted_iota(jnp.int32, (ROWS, 128), 1)

    def prepare(slot, buf, place):
        x = xb[slot, :, 0:384].astype(F32)
        sq = x * x
        nx = jnp.sum(sq[:, 0:128] + sq[:, 128:256] + sq[:, 256:384], axis=1, keepdims=True)
        hi, mid, low = split3(-0.5 * nx)
        cols = jnp.where(lane_full < 3, 1.0, 0.0)
        cols = jnp.where(lane_full == 3, hi, cols)
        cols = jnp.where(lane_full == 4, mid, cols)
        cols = jnp.where(lane_full == 5, low, cols)
        base = pl.multiple_of(place * ROWS, ROWS)
        aug[buf][pl.ds(base, ROWS), :] = cols.astype(BF16)
        w = wsm[slot * 6 + 5]
        for p in range(4, -1, -1):
            w = jnp.where(lane < PIECES[p + 1][0], wsm[slot * 6 + p], w)
        v_t = xb[slot, :, 384:512].T[0:64, :]
        stage[:, pl.ds(base, ROWS)] = (v_t.astype(F32) * w.astype(F32)).astype(BF16)

    send_own()
    mask_words(0, False)

    vt[...] = jnp.zeros_like(vt)
    stage[...] = jnp.zeros_like(stage)
    ks0[...] = jnp.zeros_like(ks0)
    ks1[...] = jnp.zeros_like(ks1)
    y_ref[...] = jnp.zeros_like(y_ref)
    z_in.wait()
    row = lax.broadcasted_iota(jnp.int32, (128, tile), 0)

    def prepare_targets(r, carry):
        base = pl.multiple_of(r * tile, tile)
        zr = zv[pl.ds(base, tile), :].T
        zt[0:384, pl.ds(base, tile)] = zr
        zf = zr.astype(F32)
        hi, mid, low = split3(-0.5 * jnp.sum(zf * zf, axis=0, keepdims=True))
        rows = jnp.where(row == 0, hi, jnp.where(row == 1, mid, jnp.where(row == 2, low, 0.0)))
        rows = jnp.where((row >= 3) & (row < 6), 1.0, rows)
        zt[384:512, pl.ds(base, tile)] = rows.astype(BF16)
        return carry

    lax.fori_loop(0, TILES, prepare_targets, 0)
    ell = jnp.full((1, tile), ell_ref[0], F32)
    rate = LOG2E / (ell * ell)
    scale = scale_ref[0]

    prepare(0, 0, 0)
    arrive(0)
    forward(0)
    to_partner(0)
    for n in range(1, ring):
        prepare(n, 0, n)

    def product(buf, ks, at):
        base = pl.multiple_of(at * tile, tile)
        y_ref[:, pl.ds(base, tile)] += jnp.dot(vt[buf], ks[...], preferred_element_type=F32)

    def run_chunk(g, prep):
        first = 2 * ring * g + (ring if g == n_groups else 0)
        count = ring if g in (0, n_groups) else 2 * ring
        rows = count * ROWS
        vt[g % 2] = stage[...]
        if g == n_groups - 1:
            stage[:, half:] = jnp.zeros((64, half), BF16)

        def block(r, ks):
            src = xb[pl.ds(first, count)].reshape(rows, 512)[:, 0:384]
            lhs = jnp.concatenate([src, aug[g % 2][0:rows, :]], axis=1)
            base = pl.multiple_of(r * tile, tile)
            neg = jnp.dot(lhs, zt[:, pl.ds(base, tile)], preferred_element_type=F32)
            val = jnp.exp2(jnp.minimum(neg * rate, 0.0)) * scale
            ks[0:rows, :] = val.astype(BF16)

        def body(m, carry):
            product(jnp.where(m == 0, (g + 1) % 2, g % 2), ks1, (2 * m + TILES - 1) % TILES)
            block(2 * m, ks0)
            if prep:
                prepare_next(g + 1, m)
            block(2 * m + 1, ks1)
            product(g % 2, ks0, 2 * m)
            return carry

        lax.fori_loop(0, TILES // 2, body, 0)

    def prepare_next(n, m):
        for u in range(per_body):
            place = m * per_body + u
            if n < n_groups:
                prepare(2 * ring * n + place, n % 2, place)
            if n >= 1:
                prepare(2 * ring * n + ring + place, n % 2, place + (0 if n == n_groups else ring))

    def communicate(n):
        if n < n_groups:
            arrive(n)
            forward(n)
            to_partner(n)
            mask_words(n, False)
        mask_words(n - 1, True)
        from_partner(n - 1)

    for g in range(n_groups + 1):
        if g == n_groups:
            run_chunk(g, False)
        elif g < EARLY:
            run_chunk(g, False)
            communicate(g + 1)

            def prep_body(m, carry, n=g + 1):
                prepare_next(n, m)
                return carry

            lax.fori_loop(0, TILES // 2, prep_body, 0)
        else:
            communicate(g + 1)
            run_chunk(g, True)
    product(n_groups % 2, ks1, TILES - 1)
    for q in range(n_groups):
        done = xb.at[pl.ds(0, sent[q])]
        pltpu.make_async_copy(done, done, send_sem.at[q]).wait()


def solution(mesh):
    devices = mesh.shape["sp"]
    ring = round((devices // 2) ** (1 / 3))
    n_groups = ring**2
    slots = 2 * ring * (n_groups + 1)
    rows = 2 * ring * ROWS
    row_spec = P(("dp", "sp"), None)

    def local_fn(z_rows, x_rows, v_rows, mask_row, length_scale, out_scale):
        targets = z_rows.shape[0]
        tile = targets // TILES
        pad = jnp.zeros((ROWS, 128 - v_rows.shape[1]), BF16)
        packed = jnp.concatenate([x_rows, v_rows, pad], axis=1)
        y_t = pl.pallas_call(
            functools.partial(kernel, ring),
            out_shape=jax.ShapeDtypeStruct((64, targets), F32),
            in_specs=[
                pl.BlockSpec(memory_space=pl.ANY),
                pl.BlockSpec(memory_space=pl.ANY),
                pl.BlockSpec(memory_space=pltpu.SMEM),
                pl.BlockSpec(memory_space=pltpu.SMEM),
                pl.BlockSpec(memory_space=pltpu.SMEM),
            ],
            out_specs=pl.BlockSpec(memory_space=pltpu.VMEM),
            scratch_shapes=[
                pltpu.VMEM((slots, ROWS, 512), BF16),
                pltpu.VMEM((targets, 384), BF16),
                pltpu.VMEM((512, targets), BF16),
                pltpu.VMEM((rows, 128), BF16),
                pltpu.VMEM((rows, 128), BF16),
                pltpu.VMEM((64, rows), BF16),
                pltpu.VMEM((2, 64, rows), BF16),
                pltpu.VMEM((rows, tile), BF16),
                pltpu.VMEM((rows, tile), BF16),
                pltpu.SMEM((slots * 6,), jnp.int32),
                pltpu.SemaphoreType.DMA((2,)),
                pltpu.SemaphoreType.DMA((n_groups,)),
                pltpu.SemaphoreType.DMA((n_groups,)),
                pltpu.SemaphoreType.DMA((n_groups,)),
            ],
            compiler_params=pltpu.CompilerParams(
                collective_id=0, has_side_effects=True, vmem_limit_bytes=60 * 2**20
            ),
            name="gather_product",
        )(packed, z_rows, mask_row, length_scale, out_scale)
        return y_t.T

    return jax.shard_map(
        local_fn,
        mesh=mesh,
        in_specs=(row_spec, row_spec, row_spec, row_spec, P(None), P(None)),
        out_specs=row_spec,
        check_vma=False,
    )
```

time: 105 us -> 86.1 us (0.82)
  Pallas kernels: 98.6 us -> 80.2 us
    pallas_call x1, Pallas kernels: 98.6 us -> 80.2 us  [local_fn(): pl.pallas_call(functools.partial(kernel, ring), out_shape=jax.ShapeDtypeS...]
where the time goes in v2:
time: 86.1 us; the launch traced here: 85.9 us
  Pallas kernels  80.2 us (93%)
  local copies, waits for them, and re-layouts  2.78 us (3%)
  other arithmetic  1.58 us (2%)
  between operations  1.32 us (2%)
    pallas_call x1, Pallas kernels, local_fn(): pl.pallas_call(functools.partial(kernel, ring), out_shape=jax.ShapeDtypeS...  80.2 us
    unnamed x2, local copies, waits for them, and re-layouts  2.7 us

profile of v2, /device:TPU:1, one launch (start us, length us, event | category | flops | bytes accessed | tf_op | source)
XLA Modules:
  0.0 85.9 jit_solution(12813286927777785289)
XLA Ops:
  1.3 0.1 pad.2.clone
  1.4 0.8 copy.7
  2.2 1.6 %maximum_maximum_fusion.x_hbm = bf16[128,512]{1,0:T(8,128)(2,1)} fusion(bf16[128,64]{1,0:T(8,128)(2,1)S(1)} %copy.7, bf16[128,384]{1,0:T(8,128)(2,1)} %param.7, bf16[512]{0:T(512)(128)(2,1)S(1)} %pad.2.clone), kind=kLoop, calls=%fused_computation | loop fusion | flops 393216 | bytes 246784 | tf_op jit(solution)/shard_map/concatenate | solution.py:271
  3.8 80.2 %gather_product.1 = f32[64,2048]{1,0:T(8,128)} custom-call(bf16[128,512]{1,0:T(8,128)(2,1)} %maximum_maximum_fusion.x_hbm, bf16[2048,384]{1,0:T(8,128)(2,1)} %z_hbm.1, s32[1,128]{1,0:T(1,128)} %w_ref.1, f32[1]{0:T(128)S(6)} %copy.9.ell_ref, f32[1]{0:T(128)S(6)} %copy.10.scale_ref), custom_call_target="tpu_custom_call" | custom-call | tf_op jit(solution)/shard_map/gather_product/pallas_call | solution.py:272
  84.0 1.9 %copy.11 = f32[2048,64]{0,1:T(8,128)} copy(f32[2048,64]{0,1:T(8,128)} %bitcast.1) | data formatting | bytes 1048576
  (1 shorter events, 0.0 us)

commit v3 on v2

--- a/solution.py
+++ b/solution.py
@@ -13,8 +13,8 @@
 LOG2E = 1.4426950408889634
 ROWS = 128
 PIECES = ((0, 32, 0, 1), (32, 16, 0, -1), (48, 32, 1, 1), (80, 16, 1, -1), (96, 16, 2, 1), (112, 16, 2, -1))
-TILES = 4
-EARLY = 1
+TILES = 2
+PART = 2
 
 
 def line_order(ring):
@@ -30,14 +30,12 @@
 
 
 def kernel(ring, x_hbm, z_hbm, w_ref, ell_ref, scale_ref, y_ref,
-           xb, zv, zt, aug0, aug1, stage, vt, ks0, ks1, wsm, in_sem, recv_sem, pair_sem, send_sem):
+           xb, zv, zt, aug, aug_next, stage, vt, ks0, ks1, wsm, in_sem, recv_sem, pair_sem, send_sem):
     order = line_order(ring)
     slot_of = {h: n for n, h in enumerate(order)}
     n_groups = len(order)
     half = ring * ROWS
     tile = zv.shape[0] // TILES
-    aug = (aug0, aug1)
-    per_body = ring // (TILES // 2)
 
     me = lax.axis_index("sp")
     core = me % 2
@@ -136,7 +134,7 @@
     lane = lax.broadcasted_iota(jnp.int32, (1, 128), 1)
     lane_full = lax.broadcasted_iota(jnp.int32, (ROWS, 128), 1)
 
-    def prepare(slot, buf, place):
+    def prepare(slot, place):
         x = xb[slot, :, 0:384].astype(F32)
         sq = x * x
         nx = jnp.sum(sq[:, 0:128] + sq[:, 128:256] + sq[:, 256:384], axis=1, keepdims=True)
@@ -145,13 +143,13 @@
         cols = jnp.where(lane_full == 3, hi, cols)
         cols = jnp.where(lane_full == 4, mid, cols)
         cols = jnp.where(lane_full == 5, low, cols)
-        base = pl.multiple_of(place * ROWS, ROWS)
-        aug[buf][pl.ds(base, ROWS), :] = cols.astype(BF16)
+        at = pl.ds(place * ROWS, ROWS)
+        aug_next[at, :] = cols.astype(BF16)
         w = wsm[slot * 6 + 5]
         for p in range(4, -1, -1):
             w = jnp.where(lane < PIECES[p + 1][0], wsm[slot * 6 + p], w)
         v_t = xb[slot, :, 384:512].T[0:64, :]
-        stage[:, pl.ds(base, ROWS)] = (v_t.astype(F32) * w.astype(F32)).astype(BF16)
+        stage[:, at] = (v_t.astype(F32) * w.astype(F32)).astype(BF16)
 
     send_own()
     mask_words(0, False)
@@ -162,69 +160,58 @@
     ks1[...] = jnp.zeros_like(ks1)
     y_ref[...] = jnp.zeros_like(y_ref)
     z_in.wait()
-    row = lax.broadcasted_iota(jnp.int32, (128, tile), 0)
+    narrow = tile // 2
+    row = lax.broadcasted_iota(jnp.int32, (128, narrow), 0)
 
     def prepare_targets(r, carry):
-        base = pl.multiple_of(r * tile, tile)
-        zr = zv[pl.ds(base, tile), :].T
-        zt[0:384, pl.ds(base, tile)] = zr
+        base = pl.multiple_of(r * narrow, narrow)
+        zr = zv[pl.ds(base, narrow), :].T
+        zt[0:384, pl.ds(base, narrow)] = zr
         zf = zr.astype(F32)
         hi, mid, low = split3(-0.5 * jnp.sum(zf * zf, axis=0, keepdims=True))
         rows = jnp.where(row == 0, hi, jnp.where(row == 1, mid, jnp.where(row == 2, low, 0.0)))
         rows = jnp.where((row >= 3) & (row < 6), 1.0, rows)
-        zt[384:512, pl.ds(base, tile)] = rows.astype(BF16)
+        zt[384:512, pl.ds(base, narrow)] = rows.astype(BF16)
         return carry
 
-    lax.fori_loop(0, TILES, prepare_targets, 0)
-    ell = jnp.full((1, tile), ell_ref[0], F32)
+    lax.fori_loop(0, 2 * TILES, prepare_targets, 0)
+    ell = jnp.full((1, 1), ell_ref[0], F32)
     rate = LOG2E / (ell * ell)
     scale = scale_ref[0]
 
-    prepare(0, 0, 0)
+    prepare(0, 0)
     arrive(0)
     forward(0)
     to_partner(0)
     for n in range(1, ring):
-        prepare(n, 0, n)
-
-    def product(buf, ks, at):
-        base = pl.multiple_of(at * tile, tile)
-        y_ref[:, pl.ds(base, tile)] += jnp.dot(vt[buf], ks[...], preferred_element_type=F32)
-
-    def run_chunk(g, prep):
-        first = 2 * ring * g + (ring if g == n_groups else 0)
-        count = ring if g in (0, n_groups) else 2 * ring
-        rows = count * ROWS
+        prepare(n, n)
+    tiles = (ks0, ks1)
+
+    def product(buf, u, part):
+        rows = slice(part * PART * ROWS, (part + 1) * PART * ROWS)
+        cols = slice(u * tile, (u + 1) * tile)
+        y_ref[:, cols] += jnp.dot(vt[buf, :, rows], tiles[u][rows, :], preferred_element_type=F32)
+
+    def block(first, u, part):
+        rows = slice(part * PART * ROWS, (part + 1) * PART * ROWS)
+        src = xb[pl.ds(first + part * PART, PART)].reshape(PART * ROWS, 512)[:, 0:384]
+        lhs = jnp.concatenate([src, aug[rows, :]], axis=1)
+        neg = jnp.dot(lhs, zt[:, u * tile:(u + 1) * tile], preferred_element_type=F32)
+        val = jnp.exp2(jnp.minimum(neg * rate, 0.0)) * scale
+        tiles[u][rows, :] = val.astype(BF16)
+
+    def run_chunk(g, parts, prep):
+        first = 2 * ring * g
         vt[g % 2] = stage[...]
-        if g == n_groups - 1:
-            stage[:, half:] = jnp.zeros((64, half), BF16)
-
-        def block(r, ks):
-            src = xb[pl.ds(first, count)].reshape(rows, 512)[:, 0:384]
-            lhs = jnp.concatenate([src, aug[g % 2][0:rows, :]], axis=1)
-            base = pl.multiple_of(r * tile, tile)
-            neg = jnp.dot(lhs, zt[:, pl.ds(base, tile)], preferred_element_type=F32)
-            val = jnp.exp2(jnp.minimum(neg * rate, 0.0)) * scale
-            ks[0:rows, :] = val.astype(BF16)
-
-        def body(m, carry):
-            product(jnp.where(m == 0, (g + 1) % 2, g % 2), ks1, (2 * m + TILES - 1) % TILES)
-            block(2 * m, ks0)
-            if prep:
-                prepare_next(g + 1, m)
-            block(2 * m + 1, ks1)
-            product(g % 2, ks0, 2 * m)
-            return carry
-
-        lax.fori_loop(0, TILES // 2, body, 0)
-
-    def prepare_next(n, m):
-        for u in range(per_body):
-            place = m * per_body + u
-            if n < n_groups:
-                prepare(2 * ring * n + place, n % 2, place)
-            if n >= 1:
-                prepare(2 * ring * n + ring + place, n % 2, place + (0 if n == n_groups else ring))
+        aug[...] = aug_next[...]
+        for u in range(TILES):
+            for part in range(ring):
+                if part in parts:
+                    block(first, u, part)
+                product((g + 1) % 2 if u == 0 else g % 2, (u + TILES - 1) % TILES, part)
+                if prep:
+                    place = u * ring + part
+                    prepare(2 * ring * (g + 1) + place, place)
 
     def communicate(n):
         if n < n_groups:
@@ -235,22 +222,31 @@
         mask_words(n - 1, True)
         from_partner(n - 1)
 
-    for g in range(n_groups + 1):
-        if g == n_groups:
-            run_chunk(g, False)
-        elif g < EARLY:
-            run_chunk(g, False)
-            communicate(g + 1)
-
-            def prep_body(m, carry, n=g + 1):
-                prepare_next(n, m)
-                return carry
-
-            lax.fori_loop(0, TILES // 2, prep_body, 0)
-        else:
-            communicate(g + 1)
-            run_chunk(g, True)
-    product(n_groups % 2, ks1, TILES - 1)
+    run_chunk(0, range(ring // PART), False)
+    communicate(1)
+    for place in range(2 * ring):
+        prepare(2 * ring + place, place)
+
+    def chunk(g, carry):
+        for low in range(1, n_groups, ring):
+            high = min(low + ring, n_groups)
+
+            @pl.when((g >= low) & (g < high))
+            def _(low=low, high=high):
+                for n in range(low, high):
+
+                    @pl.when(g == n)
+                    def _(n=n):
+                        communicate(n + 1)
+
+        run_chunk(g, range(ring), True)
+        return carry
+
+    lax.fori_loop(1, n_groups, chunk, 0)
+    stage[:, 0:half] = jnp.zeros((64, half), BF16)
+    run_chunk(n_groups, range(ring // PART, ring), False)
+    for part in range(ring):
+        product(n_groups % 2, TILES - 1, part)
     for q in range(n_groups):
         done = xb.at[pl.ds(0, sent[q])]
         pltpu.make_async_copy(done, done, send_sem.at[q]).wait()

time: 86.1 us -> 85.1 us (0.988)
  Pallas kernels: 80.2 us -> 79.1 us
    pallas_call x1, Pallas kernels: 80.2 us -> 79.1 us  [local_fn(): pl.pallas_call(functools.partial(kernel, ring), out_shape=jax.ShapeDtypeS...]
where the time goes in v3:
time: 85.1 us; the launch traced here: 84.8 us
  Pallas kernels  79.1 us (93%)
  local copies, waits for them, and re-layouts  2.78 us (3%)
  other arithmetic  1.58 us (2%)
  between operations  1.32 us (2%)
    pallas_call x1, Pallas kernels, local_fn(): pl.pallas_call(functools.partial(kernel, ring), out_shape=jax.ShapeDtypeS...  79.1 us
    unnamed x2, local copies, waits for them, and re-layouts  2.7 us

profile of v3, /device:TPU:1, one launch (start us, length us, event | category | flops | bytes accessed | tf_op | source)
XLA Modules:
  0.0 84.8 jit_solution(13893475125424127677)
XLA Ops:
  1.3 0.1 pad.2.clone
  1.4 0.8 copy.7
  2.2 1.6 %maximum_maximum_fusion.x_hbm = bf16[128,512]{1,0:T(8,128)(2,1)} fusion(bf16[128,64]{1,0:T(8,128)(2,1)S(1)} %copy.7, bf16[128,384]{1,0:T(8,128)(2,1)} %param.7, bf16[512]{0:T(512)(128)(2,1)S(1)} %pad.2.clone), kind=kLoop, calls=%fused_computation | loop fusion | flops 393216 | bytes 246784 | tf_op jit(solution)/shard_map/concatenate | solution.py:267
  3.8 79.1 %gather_product.1 = f32[64,2048]{1,0:T(8,128)} custom-call(bf16[128,512]{1,0:T(8,128)(2,1)} %maximum_maximum_fusion.x_hbm, bf16[2048,384]{1,0:T(8,128)(2,1)} %z_hbm.1, s32[1,128]{1,0:T(1,128)} %w_ref.1, f32[1]{0:T(128)S(6)} %copy.9.ell_ref, f32[1]{0:T(128)S(6)} %copy.10.scale_ref), custom_call_target="tpu_custom_call" | custom-call | tf_op jit(solution)/shard_map/gather_product/pallas_call | solution.py:268
  82.9 1.9 %copy.11 = f32[2048,64]{0,1:T(8,128)} copy(f32[2048,64]{0,1:T(8,128)} %bitcast.1) | data formatting | bytes 1048576
  (1 shorter events, 0.0 us)

commit v4 on v3

--- a/solution.py
+++ b/solution.py
@@ -29,8 +29,8 @@
     return hi, mid, (rest - mid).astype(BF16).astype(F32)
 
 
-def kernel(ring, x_hbm, z_hbm, w_ref, ell_ref, scale_ref, y_ref,
-           xb, zv, zt, aug, aug_next, stage, vt, ks0, ks1, wsm, in_sem, recv_sem, pair_sem, send_sem):
+def kernel(ring, x_hbm, v_hbm, z_hbm, w_ref, ell_ref, scale_ref, y_ref,
+           xb, zv, zt, vin, aug, aug_next, stage, vt, ks0, ks1, wsm, in_sem, line_sem, recv_sem, pair_sem, send_sem):
     order = line_order(ring)
     slot_of = {h: n for n, h in enumerate(order)}
     n_groups = len(order)
@@ -57,37 +57,43 @@
 
     partner = me + step
 
-    own_in = pltpu.make_async_copy(x_hbm, xb.at[0], in_sem.at[0])
+    own_in = pltpu.make_async_copy(x_hbm, xb.at[0, :, pl.ds(0, 384)], in_sem.at[0])
+    v_in = pltpu.make_async_copy(v_hbm, vin, in_sem.at[2])
     z_in = pltpu.make_async_copy(z_hbm, zv, in_sem.at[1])
+    v_in.start()
     own_in.start()
     z_in.start()
     barrier = pltpu.get_barrier_semaphore()
     others = [downstream(axis, 1, hop) for axis in range(3) for hop in range(1, ring)] + [partner]
     for other in others:
         pl.semaphore_signal(barrier, inc=1, device_id={"sp": other}, device_id_type=MESH)
+    v_in.wait()
+    xb[0, :, 384:512] = jnp.concatenate([vin[...], jnp.zeros_like(vin)], axis=0).T
     pl.semaphore_wait(barrier, len(others))
     own_in.wait()
 
     sent = [0] * n_groups
-
-    def send(src, dst, axis, sign, hop, q, m):
+    nearest = sorted(range(1, ring), key=lambda h: min(h, ring - h))
+
+    def send(src, dst, axis, sign, hop, q, landed):
         pltpu.make_async_remote_copy(
             src_ref=src,
             dst_ref=dst,
             send_sem=send_sem.at[q],
-            recv_sem=recv_sem.at[m],
+            recv_sem=landed,
             device_id={"sp": downstream(axis, sign, hop)},
             device_id_type=MESH,
         ).start()
 
     def send_own():
-        for hop in sorted(range(1, ring), key=lambda h: min(h, ring - h)):
+        for hop in nearest:
             for lo, cnt, rot, sign in PIECES:
                 rows = pl.ds(lo, cnt)
-                send(xb.at[0, rows], xb.at[hop, rows], rot, sign, hop, 0, 0)
+                send(xb.at[0, rows], xb.at[hop, rows], rot, sign, hop, 0, line_sem.at[hop])
             sent[0] += 1
 
-    def forward(q):
+    def forward(q, i=None):
+        here, count = (0, ring) if i is None else (i, 1)
         j, k = order[q]
         for leg, child in ((1, (j + 1, k) if k == 0 else None), (2, (j, k + 1))):
             if child not in slot_of:
@@ -96,14 +102,14 @@
             for lo, cnt, rot, sign in PIECES:
                 rows = pl.ds(lo, cnt)
                 send(
-                    xb.at[pl.ds(2 * ring * q, ring), rows],
-                    xb.at[pl.ds(2 * ring * m, ring), rows],
-                    (rot + leg) % 3, sign, 1, q, m,
+                    xb.at[pl.ds(2 * ring * q + here, count), rows],
+                    xb.at[pl.ds(2 * ring * m + here, count), rows],
+                    (rot + leg) % 3, sign, 1, q, recv_sem.at[m],
                 )
-            sent[q] += ring
+            sent[q] += count
 
     def arrive(q):
-        dst = xb.at[pl.ds(1, ring - 1)] if q == 0 else xb.at[pl.ds(2 * ring * q, ring)]
+        dst = xb.at[pl.ds(2 * ring * q, ring)]
         pltpu.make_async_copy(dst, dst, recv_sem.at[q]).wait()
 
     def to_partner(q):
@@ -152,6 +158,7 @@
         stage[:, at] = (v_t.astype(F32) * w.astype(F32)).astype(BF16)
 
     send_own()
+    forward(0, 0)
     mask_words(0, False)
 
     vt[...] = jnp.zeros_like(vt)
@@ -180,8 +187,10 @@
     scale = scale_ref[0]
 
     prepare(0, 0)
-    arrive(0)
-    forward(0)
+    for hop in nearest:
+        dst = xb.at[hop]
+        pltpu.make_async_copy(dst, dst, line_sem.at[hop]).wait()
+        forward(0, hop)
     to_partner(0)
     for n in range(1, ring):
         prepare(n, n)
@@ -263,12 +272,11 @@
     def local_fn(z_rows, x_rows, v_rows, mask_row, length_scale, out_scale):
         targets = z_rows.shape[0]
         tile = targets // TILES
-        pad = jnp.zeros((ROWS, 128 - v_rows.shape[1]), BF16)
-        packed = jnp.concatenate([x_rows, v_rows, pad], axis=1)
         y_t = pl.pallas_call(
             functools.partial(kernel, ring),
             out_shape=jax.ShapeDtypeStruct((64, targets), F32),
             in_specs=[
+                pl.BlockSpec(memory_space=pl.ANY),
                 pl.BlockSpec(memory_space=pl.ANY),
                 pl.BlockSpec(memory_space=pl.ANY),
                 pl.BlockSpec(memory_space=pltpu.SMEM),
@@ -280,6 +288,7 @@
                 pltpu.VMEM((slots, ROWS, 512), BF16),
                 pltpu.VMEM((targets, 384), BF16),
                 pltpu.VMEM((512, targets), BF16),
+                pltpu.VMEM((64, ROWS), BF16),
                 pltpu.VMEM((rows, 128), BF16),
                 pltpu.VMEM((rows, 128), BF16),
                 pltpu.VMEM((64, rows), BF16),
@@ -287,7 +296,8 @@
                 pltpu.VMEM((rows, tile), BF16),
                 pltpu.VMEM((rows, tile), BF16),
                 pltpu.SMEM((slots * 6,), jnp.int32),
-                pltpu.SemaphoreType.DMA((2,)),
+                pltpu.SemaphoreType.DMA((3,)),
+                pltpu.SemaphoreType.DMA((ring,)),
                 pltpu.SemaphoreType.DMA((n_groups,)),
                 pltpu.SemaphoreType.DMA((n_groups,)),
                 pltpu.SemaphoreType.DMA((n_groups,)),
@@ -296,7 +306,7 @@
                 collective_id=0, has_side_effects=True, vmem_limit_bytes=60 * 2**20
             ),
             name="gather_product",
-        )(packed, z_rows, mask_row, length_scale, out_scale)
+        )(x_rows, v_rows.T, z_rows, mask_row, length_scale, out_scale)
         return y_t.T
 
     return jax.shard_map(

time: 85.1 us -> 82.1 us (0.965)
  other arithmetic: 1.58 us -> 0 us
  local copies, waits for them, and re-layouts: 2.78 us -> 1.87 us
    concatenate x1 -> x0, other arithmetic: 1.58 us -> none  [local_fn(): packed = jnp.concatenate([x_rows, v_rows, pad], axis=1)]
    unnamed x2 -> x1, local copies, waits for them, and re-layouts: 2.7 us -> 1.87 us
where the time goes in v4:
time: 82.1 us; the launch traced here: 81.9 us
  Pallas kernels  78.7 us (96%)
  local copies, waits for them, and re-layouts  1.87 us (2%)
  between operations  1.3 us (2%)
    pallas_call x1, Pallas kernels, local_fn(): pl.pallas_call(functools.partial(kernel, ring), out_shape=jax.ShapeDtypeS...  78.7 us
    unnamed x1, local copies, waits for them, and re-layouts  1.87 us

profile of v4, /device:TPU:1, one launch (start us, length us, event | category | flops | bytes accessed | tf_op | source)
XLA Modules:
  0.0 81.9 jit_solution(5982841634734436743)
XLA Ops:
  1.3 78.7 %gather_product.1 = f32[64,2048]{1,0:T(8,128)} custom-call(bf16[128,384]{1,0:T(8,128)(2,1)} %x_hbm.1, bf16[64,128]{1,0:T(8,128)(2,1)} %bitcast.3, bf16[2048,384]{1,0:T(8,128)(2,1)} %z_hbm.1, s32[1,128]{1,0:T(1,128)} %w_ref.1, f32[1]{0:T(128)S(6)} %copy.8.ell_ref, f32[1]{0:T(128)S(6)} %copy.9.scale_ref), custom_call_target="tpu_custom_call" | custom-call | tf_op jit(solution)/shard_map/gather_product/pallas_call | solution.py:275
  80.0 1.9 %copy.10 = f32[2048,64]{0,1:T(8,128)} copy(f32[2048,64]{0,1:T(8,128)} %bitcast.2) | data formatting | bytes 1048576

commit v5 on v4

--- a/solution.py
+++ b/solution.py
@@ -30,7 +30,7 @@
 
 
 def kernel(ring, x_hbm, v_hbm, z_hbm, w_ref, ell_ref, scale_ref, y_ref,
-           xb, zv, zt, vin, aug, aug_next, stage, vt, ks0, ks1, wsm, in_sem, line_sem, recv_sem, pair_sem, send_sem):
+           xb, zv, zt, vin, aug0, aug1, stage, vt, ks0, ks1, wsm, in_sem, line_sem, recv_sem, pair_sem, send_sem):
     order = line_order(ring)
     slot_of = {h: n for n, h in enumerate(order)}
     n_groups = len(order)
@@ -140,7 +140,9 @@
     lane = lax.broadcasted_iota(jnp.int32, (1, 128), 1)
     lane_full = lax.broadcasted_iota(jnp.int32, (ROWS, 128), 1)
 
-    def prepare(slot, place):
+    aug = (aug0, aug1)
+
+    def prepare(slot, place, parity):
         x = xb[slot, :, 0:384].astype(F32)
         sq = x * x
         nx = jnp.sum(sq[:, 0:128] + sq[:, 128:256] + sq[:, 256:384], axis=1, keepdims=True)
@@ -150,7 +152,7 @@
         cols = jnp.where(lane_full == 4, mid, cols)
         cols = jnp.where(lane_full == 5, low, cols)
         at = pl.ds(place * ROWS, ROWS)
-        aug_next[at, :] = cols.astype(BF16)
+        aug[parity][at, :] = cols.astype(BF16)
         w = wsm[slot * 6 + 5]
         for p in range(4, -1, -1):
             w = jnp.where(lane < PIECES[p + 1][0], wsm[slot * 6 + p], w)
@@ -186,14 +188,14 @@
     rate = LOG2E / (ell * ell)
     scale = scale_ref[0]
 
-    prepare(0, 0)
+    prepare(0, 0, 0)
     for hop in nearest:
         dst = xb.at[hop]
         pltpu.make_async_copy(dst, dst, line_sem.at[hop]).wait()
         forward(0, hop)
     to_partner(0)
     for n in range(1, ring):
-        prepare(n, n)
+        prepare(n, n, 0)
     tiles = (ks0, ks1)
 
     def product(buf, u, part):
@@ -201,26 +203,25 @@
         cols = slice(u * tile, (u + 1) * tile)
         y_ref[:, cols] += jnp.dot(vt[buf, :, rows], tiles[u][rows, :], preferred_element_type=F32)
 
-    def block(first, u, part):
+    def block(first, u, part, parity):
         rows = slice(part * PART * ROWS, (part + 1) * PART * ROWS)
         src = xb[pl.ds(first + part * PART, PART)].reshape(PART * ROWS, 512)[:, 0:384]
-        lhs = jnp.concatenate([src, aug[rows, :]], axis=1)
+        lhs = jnp.concatenate([src, aug[parity][rows, :]], axis=1)
         neg = jnp.dot(lhs, zt[:, u * tile:(u + 1) * tile], preferred_element_type=F32)
         val = jnp.exp2(jnp.minimum(neg * rate, 0.0)) * scale
         tiles[u][rows, :] = val.astype(BF16)
 
-    def run_chunk(g, parts, prep):
+    def run_chunk(g, parts, prep, parity):
         first = 2 * ring * g
-        vt[g % 2] = stage[...]
-        aug[...] = aug_next[...]
+        vt[parity] = stage[...]
         for u in range(TILES):
             for part in range(ring):
                 if part in parts:
-                    block(first, u, part)
-                product((g + 1) % 2 if u == 0 else g % 2, (u + TILES - 1) % TILES, part)
+                    block(first, u, part, parity)
+                product(1 - parity if u == 0 else parity, (u + TILES - 1) % TILES, part)
                 if prep:
                     place = u * ring + part
-                    prepare(2 * ring * (g + 1) + place, place)
+                    prepare(2 * ring * (g + 1) + place, place, 1 - parity)
 
     def communicate(n):
         if n < n_groups:
@@ -231,29 +232,34 @@
         mask_words(n - 1, True)
         from_partner(n - 1)
 
-    run_chunk(0, range(ring // PART), False)
+    run_chunk(0, range(ring // PART), False, 0)
     communicate(1)
     for place in range(2 * ring):
-        prepare(2 * ring + place, place)
-
-    def chunk(g, carry):
-        for low in range(1, n_groups, ring):
-            high = min(low + ring, n_groups)
-
-            @pl.when((g >= low) & (g < high))
-            def _(low=low, high=high):
-                for n in range(low, high):
-
-                    @pl.when(g == n)
-                    def _(n=n):
-                        communicate(n + 1)
-
-        run_chunk(g, range(ring), True)
+        prepare(2 * ring + place, place, 1)
+
+    def chunk_pair(m, carry):
+        for parity in (1, 0):
+            g = 2 * m + 2 - parity
+            for low in range(2 - parity, n_groups, 2 * ring):
+                high = min(low + 2 * ring, n_groups)
+
+                @pl.when((g >= low) & (g < high))
+                def _(low=low, high=high, g=g):
+                    for n in range(low, high, 2):
+                        if n < n_groups - 1:
+
+                            @pl.when(g == n)
+                            def _(n=n):
+                                communicate(n + 1)
+
+            run_chunk(g, range(ring), True, parity)
         return carry
 
-    lax.fori_loop(1, n_groups, chunk, 0)
+    lax.fori_loop(0, n_groups // 2 - 1, chunk_pair, 0)
+    communicate(n_groups)
+    run_chunk(n_groups - 1, range(ring), True, 1)
     stage[:, 0:half] = jnp.zeros((64, half), BF16)
-    run_chunk(n_groups, range(ring // PART, ring), False)
+    run_chunk(n_groups, range(ring // PART, ring), False, n_groups % 2)
     for part in range(ring):
         product(n_groups % 2, TILES - 1, part)
     for q in range(n_groups):

time: 82.1 us -> 81.3 us (level)
  no operation moved by 1% of the time
where the time goes in v5:
time: 81.3 us; the launch traced here: 81.1 us
  Pallas kernels  78 us (96%)
  local copies, waits for them, and re-layouts  1.87 us (2%)
  between operations  1.31 us (2%)
    pallas_call x1, Pallas kernels, local_fn(): pl.pallas_call(functools.partial(kernel, ring), out_shape=jax.ShapeDtypeS...  78 us
    unnamed x1, local copies, waits for them, and re-layouts  1.87 us

profile of v5, /device:TPU:1, one launch (start us, length us, event | category | flops | bytes accessed | tf_op | source)
XLA Modules:
  0.0 81.1 jit_solution(8186121103028762749)
XLA Ops:
  1.3 78.0 %gather_product.1 = f32[64,2048]{1,0:T(8,128)} custom-call(bf16[128,384]{1,0:T(8,128)(2,1)} %x_hbm.1, bf16[64,128]{1,0:T(8,128)(2,1)} %bitcast.3, bf16[2048,384]{1,0:T(8,128)(2,1)} %z_hbm.1, s32[1,128]{1,0:T(1,128)} %w_ref.1, f32[1]{0:T(128)S(6)} %copy.8.ell_ref, f32[1]{0:T(128)S(6)} %copy.9.scale_ref), custom_call_target="tpu_custom_call" | custom-call | tf_op jit(solution)/shard_map/gather_product/pallas_call | solution.py:281
  79.3 1.9 %copy.10 = f32[2048,64]{0,1:T(8,128)} copy(f32[2048,64]{0,1:T(8,128)} %bitcast.2) | data formatting | bytes 1048576
